TPU v7x, 128 devices: a whole 4x4x4 slice. The times are simulated.
128 devices in a mesh: owner: 4 (over x), rows: 32 (over z, y, core).
Axes of the slice: x: 4, y: 4, z: 4, core: 2. Of those that a mesh axis runs over, the one named last changes fastest.
Arguments:
- w_gate: float32 [64, 2048, 1024], P('owner', 'rows'), may hold values from -0.25 to 0.25
- avg_gate: bfloat16 [64, 2048, 1024], P('owner', 'rows'), may hold values from -0.0625 to 0.0625
- w_up: float32 [64, 2048, 1024], P('owner', 'rows'), may hold values from -0.25 to 0.25
- avg_up: bfloat16 [64, 2048, 1024], P('owner', 'rows'), may hold values from -0.0625 to 0.0625
- w_down: float32 [64, 1024, 2048], P('owner', None, 'rows'), may hold values from -0.375 to 0.375
- avg_down: bfloat16 [64, 1024, 2048], P('owner', None, 'rows'), may hold values from -0.09375 to 0.09375
- router_weight: float32 [2048, 64], P('rows', 'owner'), may hold values from -0.125 to 0.125
- router_gain: float32 [2048], P('rows'), may hold values from 0.25 to 1.75
Outputs:
- serve_gate: bfloat16 [64, 2048, 1024], P('owner', None, 'rows')
- serve_up: bfloat16 [64, 2048, 1024], P('owner', None, 'rows')
- serve_down: bfloat16 [64, 1024, 2048], P('owner', 'rows')
- scale_gate: float32 [64, 1024], P('owner', 'rows')
- scale_up: float32 [64, 1024], P('owner', 'rows')
- scale_down: float32 [64, 1024], P('owner', 'rows')
- serve_router: bfloat16 [2048, 64], replicated
All inputs are finite; a program needn't handle non-finite values.
Results may differ from a plain program's by a relative error of at most 0.0015.
Values may be sent and summed in bfloat16 or wider, within the bound.
A program may use at most 128 MiB of HBM per device.

v0:
```python
import jax
import jax.numpy as jnp
from jax import lax
from jax.sharding import PartitionSpec as P


def rows_for(lines, length):
    spare = -len(lines) % length
    return jnp.pad(lines, [(0, spare)] + [(0, 0)] * (lines.ndim - 1))


def from_everyone(value, axis):
    copies = jnp.broadcast_to(value, (lax.axis_size(axis), *value.shape))
    return lax.all_to_all(copies, axis, split_axis=0, concat_axis=0, tiled=True)


def in_order(parts, dim):
    parts = jnp.moveaxis(parts, 0, dim)
    shape = parts.shape
    return parts.reshape(*shape[:dim], shape[dim] * shape[dim + 1], *shape[dim + 2 :])


def gather_directly(value, axis, dim):
    parts = from_everyone(value, axis)
    return in_order(parts, dim)


def in_blocks(value, dim, length):
    before, after = (value.shape[:dim], value.shape[dim + 1 :])
    return jnp.moveaxis(value.reshape(*before, length, -1, *after), dim, 0)


def sent_and_summed(value, axis, dim):
    length = lax.axis_size(axis)
    parts = lax.all_to_all(in_blocks(value, dim, length), axis, 0, 0, tiled=True)
    return jnp.sum(parts, axis=0)


def sum_by_parts(value, axes):
    padded = rows_for(value, lax.axis_size(axes))
    whole = gather_directly(sent_and_summed(padded, axes, 0), axes, 0)
    return lax.slice_in_dim(whole, 0, len(value)).reshape(value.shape)


def in_one(arrays, axis):
    flat, at, outs = (jnp.concatenate([a.reshape(-1) for a in arrays]), 0, [])
    total = sum_by_parts(flat, axis)
    for a in arrays:
        outs.append(total[at : at + a.size].reshape(a.shape))
        at += a.size
    return tuple(outs)


def in_one_piece(arrays, axis, split_dim, concat_dim, along):
    both = jnp.concatenate(arrays, axis=along)
    filled, at, outs = (
        lax.all_to_all(both, axis, split_axis=split_dim, concat_axis=concat_dim, tiled=True),
        0,
        [],
    )
    for a in arrays:
        outs.append(lax.slice_in_dim(filled, at, at + a.shape[along], axis=along))
        at += a.shape[along]
    return tuple(outs)


def shards(w_gate, avg_gate, w_up, avg_up, w_down, avg_down, router_weight, router_gain):
    fresh_gate = w_gate + avg_gate.astype(jnp.float32)
    fresh_up = w_up + avg_up.astype(jnp.float32)
    fresh_down = w_down + avg_down.astype(jnp.float32)
    total_gate, total_up, total_down = in_one(
        (
            jnp.sum(fresh_gate * fresh_gate, axis=1),
            jnp.sum(fresh_up * fresh_up, axis=1),
            jnp.sum(fresh_down * fresh_down, axis=2),
        ),
        "rows",
    )
    scale_gate = jnp.sqrt(total_gate)
    scale_up = jnp.sqrt(total_up)
    scale_down = jnp.sqrt(total_down)
    narrow_gate, narrow_up, narrow_down = (
        (fresh_gate / jnp.expand_dims(scale_gate, 1)).astype(jnp.bfloat16),
        (fresh_up / jnp.expand_dims(scale_up, 1)).astype(jnp.bfloat16),
        (fresh_down / jnp.expand_dims(scale_down, 2)).astype(jnp.bfloat16),
    )
    serve_gate, serve_up = in_one_piece((narrow_gate, narrow_up), "rows", 2, 1, 0)
    serve_down = lax.all_to_all(narrow_down, "rows", split_axis=1, concat_axis=2, tiled=True)
    scale_gate = lax.dynamic_slice_in_dim(
        scale_gate, lax.axis_index("rows") * serve_gate.shape[2], serve_gate.shape[2], axis=1
    )
    scale_up = lax.dynamic_slice_in_dim(
        scale_up, lax.axis_index("rows") * serve_up.shape[2], serve_up.shape[2], axis=1
    )
    scale_down = lax.dynamic_slice_in_dim(
        scale_down, lax.axis_index("rows") * serve_down.shape[1], serve_down.shape[1], axis=1
    )
    part_router = (router_weight * router_gain[:, None]).astype(jnp.bfloat16)
    row_router = gather_directly(part_router, "rows", 0)
    serve_router = gather_directly(row_router, "owner", 1)
    return (serve_gate, serve_up, serve_down, scale_gate, scale_up, scale_down, serve_router)


def solution(mesh):
    return jax.shard_map(
        shards,
        mesh=mesh,
        in_specs=(
            P("owner", "rows", None),
            P("owner", "rows", None),
            P("owner", "rows", None),
            P("owner", "rows", None),
            P("owner", None, "rows"),
            P("owner", None, "rows"),
            P("rows", "owner"),
            P("rows"),
        ),
        out_specs=(
            P("owner", None, "rows"),
            P("owner", None, "rows"),
            P("owner", "rows", None),
            P("owner", "rows"),
            P("owner", "rows"),
            P("owner", "rows"),
            P(),
        ),
        check_vma=False,
    )
```

profile of v0, /device:TPU:2, one launch (start us, length us, event | category | flops | bytes accessed | tf_op | source)
XLA Modules:
  0.0 228.1 jit_solution(5259433922244014177)
XLA Ops:
  0.6 0.0 copy-start.1
  0.6 0.0 copy-start.3
  0.7 3.8 %multiply_reduce_fusion.2 = f32[16,1024]{1,0:T(8,128)S(1)} fusion(f32[16,64,1024]{2,1,0:T(8,128)} %param.8, bf16[16,64,1024]{2,1,0:T(8,128)(2,1)} %param.9), kind=kLoop, calls=%fused_computation.8 | loop fusion | flops 4177920 | bytes 6356992 | tf_op jit(solution)/shard_map/reduce_sum | solution.py:73
  4.5 0.0 copy-start
  4.5 0.0 copy-start.2
  4.5 0.2 copy-done.1
  4.7 0.7 copy-done.3
  5.4 0.8 multiply_reduce_fusion.1
  6.2 0.0 copy-start.4
  6.2 0.0 copy-start.5
  6.2 0.6 copy-done
  6.9 0.6 copy-done.2
  7.5 0.8 multiply_reduce_fusion
  8.3 0.7 pad_maximum_fusion.1
  9.0 8.3 %all-to-all-start = ((f32[32,1,1536]{2,1,0:T(1,128)}), f32[32,1,1536]{2,1,0:T(1,128)S(1)}, u32[]{:S(2)}, u32[]{:S(2)}) async-start(f32[32,1,1536]{2,1,0:T(1,128)} %bitcast), calls=%async_computation | async-start | bytes 393216 | tf_op jit(solution)/shard_map/all_to_all | solution.py:35
  17.3 0.0 copy-done.4
  17.3 0.0 copy-done.5
  17.4 0.8 reshape.64
  18.1 7.3 %all-to-all-done = f32[32,1,1536]{2,1,0:T(1,128)S(1)} async-done(((f32[32,1,1536]{2,1,0:T(1,128)}), f32[32,1,1536]{2,1,0:T(1,128)S(1)}, u32[]{:S(2)}, u32[]{:S(2)}) %all-to-all-start) | async-done | bytes 196640 | tf_op jit(solution)/shard_map/all_to_all | solution.py:35
  25.5 3.9 %all-to-all-start.4 = ((bf16[32,2,512]{2,1,0:T(2,128)(2,1)}), bf16[32,2,512]{2,1,0:T(2,128)(2,1)S(1)}, u32[]{:S(2)}, u32[]{:S(2)}) async-start(bf16[32,2,512]{2,1,0:T(2,128)(2,1)} %reshape.64), calls=%async_computation.4 | async-start | bytes 131072 | tf_op jit(solution)/shard_map/all_to_all | solution.py:14
  29.4 0.1 reduce_sum.39
  29.5 7.4 %all-to-all-done.4 = bf16[32,2,512]{2,1,0:T(2,128)(2,1)S(1)} async-done(((bf16[32,2,512]{2,1,0:T(2,128)(2,1)}), bf16[32,2,512]{2,1,0:T(2,128)(2,1)S(1)}, u32[]{:S(2)}, u32[]{:S(2)}) %all-to-all-start.4) | async-done | bytes 65568 | tf_op jit(solution)/shard_map/all_to_all | solution.py:14
  36.8 0.8 broadcast_in_dim.6
  37.6 3.9 %all-to-all-start.1 = ((f32[32,1,1536]{2,1,0:T(1,128)}), f32[32,1,1536]{2,1,0:T(1,128)S(1)}, u32[]{:S(2)}, u32[]{:S(2)}) async-start(f32[32,1,1536]{2,1,0:T(1,128)} %broadcast_in_dim.6), calls=%async_computation.1 | async-start | bytes 393216 | tf_op jit(solution)/shard_map/all_to_all | solution.py:14
  41.5 0.1 reshape.65
  41.7 0.2 reshape.57
  41.9 7.8 %all-to-all-done.1 = f32[32,1,1536]{2,1,0:T(1,128)S(1)} async-done(((f32[32,1,1536]{2,1,0:T(1,128)}), f32[32,1,1536]{2,1,0:T(1,128)S(1)}, u32[]{:S(2)}, u32[]{:S(2)}) %all-to-all-start.1) | async-done | bytes 196640 | tf_op jit(solution)/shard_map/all_to_all | solution.py:14
  49.7 0.7 broadcast_in_dim.15
  50.4 4.8 %all-to-all-start.5 = ((bf16[4,2048,16]{1,2,0:T(8,128)(2,1)}), bf16[4,2048,16]{1,2,0:T(8,128)(2,1)S(1)}, u32[]{:S(2)}, u32[]{:S(2)}) async-start(bf16[4,2048,16]{1,2,0:T(8,128)(2,1)} %broadcast_in_dim.15), calls=%async_computation.5 | async-start | bytes 524288 | tf_op jit(solution)/shard_map/all_to_all | solution.py:14
  55.2 0.5 reduce.1
  55.7 0.1 slice.26
  55.7 0.1 slice_sqrt_fusion
  55.8 4.4 %divide_convert_fusion = bf16[16,1024,64]{1,2,0:T(8,128)(2,1)} fusion(f32[16,1024,64]{1,2,0:T(8,128)} %param.12, bf16[16,1024,64]{1,2,0:T(8,128)(2,1)S(1)} %copy-done.2, f32[16,1024]{1,0:T(8,128)S(1)} %get-tuple-element.9), kind=kLoop, calls=%fused_computation.1 | loop fusion | flops 4194304 | bytes 8454144 | tf_op jit(solution)/shard_map/convert_element_type | solution.py:85
  60.2 6.2 %copy.142 = bf16[16,1024,64]{2,0,1:T(8,128)(2,1)} copy(bf16[16,1024,64]{1,2,0:T(8,128)(2,1)} %divide_convert_fusion) | data formatting | bytes 4194304 | tf_op jit(solution)/shard_map/convert_element_type | solution.py:85
  66.4 7.9 %reshape.62 = bf16[32,2,16384]{2,1,0:T(2,128)(2,1)} reshape(bf16[1024,16,64]{2,1,0:T(8,128)(2,1)} %bitcast.38) | data formatting | bytes 4194304
  74.2 0.0 all-to-all-done.5
  74.2 4.2 %all-to-all-start.3 = ((bf16[32,2,16384]{2,1,0:T(2,128)(2,1)}), bf16[32,2,16384]{2,1,0:T(2,128)(2,1)S(1)}, u32[]{:S(2)}, u32[]{:S(2)}) async-start(bf16[32,2,16384]{2,1,0:T(2,128)(2,1)} %reshape.62), calls=%async_computation.3 | async-start | bytes 4194304 | tf_op jit(solution)/shard_map/all_to_all | solution.py:88
  78.4 6.3 %divide_convert_fusion.1 = (bf16[16,64,1024]{2,1,0:T(8,128)(2,1)S(1)}, bf16[16,64,1024]{2,1,0:T(8,128)(2,1)S(1)}) fusion(f32[16,64,1024]{2,1,0:T(8,128)} %param.10, bf16[16,64,1024]{2,1,0:T(8,128)(2,1)} %param.11, f32[16,1024]{1,0:T(8,128)S(1)} %get-tuple-element.10, f32[16,1024]{1,0:T(8,128)S(1)} %get-tuple-element.11, f32[16,64,1024]{2,1,0:T(8,128)} %param.8, ...), kind=kLoop, calls=%fused_computation.2 | loop fusion | flops 8388608 | bytes 16908288 | tf_op jit(solution)/shard_map/convert_element_type | solution.py:84
  84.7 2.3 %pad_maximum_fusion = bf16[32,64,1024]{2,1,0:T(8,128)(2,1)} fusion(bf16[16,64,1024]{2,1,0:T(8,128)(2,1)S(1)} %get-tuple-element.12, bf16[16,64,1024]{2,1,0:T(8,128)(2,1)S(1)} %get-tuple-element.13), kind=kLoop, calls=%fused_computation | loop fusion | flops 2097152 | bytes 8388608 | tf_op jit(solution)/shard_map/concatenate | solution.py:55
  87.1 12.9 %copy.138 = bf16[32,64,1024]{1,0,2:T(8,128)(2,1)} copy(bf16[32,64,1024]{2,1,0:T(8,128)(2,1)} %pad_maximum_fusion) | data formatting | bytes 8388608 | tf_op jit(solution)/shard_map/concatenate | solution.py:55
  100.0 13.9 %reshape.60 = bf16[32,2,32768]{2,1,0:T(2,128)(2,1)} reshape(bf16[1024,32,64]{2,1,0:T(8,128)(2,1)} %bitcast.35) | data formatting | bytes 8388608
  113.9 0.0 all-to-all-done.3
  113.9 7.3 %all-to-all-start.2 = ((bf16[32,2,32768]{2,1,0:T(2,128)(2,1)}), bf16[32,2,32768]{2,1,0:T(2,128)(2,1)}, u32[]{:S(2)}, u32[]{:S(2)}) async-start(bf16[32,2,32768]{2,1,0:T(2,128)(2,1)} %reshape.60), calls=%async_computation.2 | async-start | bytes 8388608 | tf_op jit(solution)/shard_map/all_to_all | solution.py:57
  121.2 0.7 constant_dynamic-slice_fusion.2
  121.9 0.7 constant_dynamic-slice_fusion
  122.6 4.0 %reshape.63 = bf16[1024,16,64]{2,1,0:T(8,128)(2,1)} reshape(bf16[32,2,16384]{2,1,0:T(2,128)(2,1)S(1)} %all-to-all-done.3) | data formatting | bytes 4194304
  126.6 6.9 %copy.144 = bf16[16,32,32,64]{3,2,1,0:T(8,128)(2,1)} copy(bf16[16,32,32,64]{3,0,1,2:T(8,128)(2,1)} %bitcast.39) | data formatting | bytes 4194304 | tf_op jit(solution)/shard_map/all_to_all | solution.py:88
  133.5 6.7 %all_to_all.49 = bf16[16,32,2048]{2,1,0:T(8,128)(2,1)} reshape(bf16[16,32,32,64]{3,2,1,0:T(8,128)(2,1)} %copy.144) | data formatting | bytes 4194304 | tf_op jit(solution)/shard_map/all_to_all | solution.py:88
  140.2 35.0 %all-to-all-done.2 = bf16[32,2,32768]{2,1,0:T(2,128)(2,1)} async-done(((bf16[32,2,32768]{2,1,0:T(2,128)(2,1)}), bf16[32,2,32768]{2,1,0:T(2,128)(2,1)}, u32[]{:S(2)}, u32[]{:S(2)}) %all-to-all-start.2) | async-done | bytes 4194336 | tf_op jit(solution)/shard_map/all_to_all | solution.py:57
  175.2 13.6 %reshape.61 = bf16[1024,32,64]{2,1,0:T(8,128)(2,1)} reshape(bf16[32,2,32768]{2,1,0:T(2,128)(2,1)} %all-to-all-done.2) | data formatting | bytes 8388608
  188.8 9.8 %copy.139 = bf16[32,64,1024]{1,2,0:T(8,128)(2,1)} copy(bf16[32,64,1024]{1,0,2:T(8,128)(2,1)} %bitcast.37) | data formatting | bytes 8388608 | tf_op jit(solution)/shard_map/all_to_all | solution.py:57
  198.6 5.6 %fusion = (bf16[16,32,64,32]{2,3,1,0:T(8,128)(2,1)}, bf16[16,32,64,32]{2,3,1,0:T(8,128)(2,1)S(1)}) fusion(bf16[32,32,64,32]{2,3,1,0:T(8,128)(2,1)} %bitcast.36), kind=kLoop, calls=%fused_computation.18 | loop fusion | bytes 8388608 | tf_op jit(solution)/shard_map/slice | solution.py:62
  204.2 3.7 %copy.140 = bf16[16,32,64,32]{2,1,3,0:T(8,128)(2,1)} copy(bf16[16,32,64,32]{2,3,1,0:T(8,128)(2,1)S(1)} %get-tuple-element.8) | data formatting | bytes 4194304 | tf_op jit(solution)/shard_map/slice | solution.py:62
  207.9 6.8 %slice.30 = bf16[16,2048,32]{1,2,0:T(8,128)(2,1)} reshape(bf16[16,32,64,32]{2,1,3,0:T(8,128)(2,1)} %copy.140) | data formatting | bytes 4194304 | tf_op jit(solution)/shard_map/slice | solution.py:62
  214.7 5.9 %copy.141 = bf16[16,32,64,32]{2,1,3,0:T(8,128)(2,1)} copy(bf16[16,32,64,32]{2,3,1,0:T(8,128)(2,1)} %get-tuple-element.7) | data formatting | bytes 4194304 | tf_op jit(solution)/shard_map/slice | solution.py:62
  220.6 6.7 %slice.32 = bf16[16,2048,32]{1,2,0:T(8,128)(2,1)} reshape(bf16[16,32,64,32]{2,1,3,0:T(8,128)(2,1)} %copy.141) | data formatting | bytes 4194304 | tf_op jit(solution)/shard_map/slice | solution.py:62
  227.4 0.7 copy.155
  (6 shorter events, 0.1 us)
Async XLA Ops:
  0.6 4.1 %copy-start.1 = (f32[16,64,1024]{2,1,0:T(8,128)S(1)}, f32[16,64,1024]{2,1,0:T(8,128)}, u32[]{:S(2)}) copy-start(f32[16,64,1024]{2,1,0:T(8,128)} %param.10) | copy-start | bytes 12582916
  0.6 4.7 %copy-start.3 = (bf16[16,64,1024]{2,1,0:T(8,128)(2,1)S(1)}, bf16[16,64,1024]{2,1,0:T(8,128)(2,1)}, u32[]{:S(2)}) copy-start(bf16[16,64,1024]{2,1,0:T(8,128)(2,1)} %param.11) | copy-start | bytes 6291460
  4.5 2.4 %copy-start = (f32[16,1024,64]{1,2,0:T(8,128)S(1)}, f32[16,1024,64]{1,2,0:T(8,128)}, u32[]{:S(2)}) copy-start(f32[16,1024,64]{1,2,0:T(8,128)} %param.12) | copy-start | bytes 12582916
  4.5 3.0 %copy-start.2 = (bf16[16,1024,64]{1,2,0:T(8,128)(2,1)S(1)}, bf16[16,1024,64]{1,2,0:T(8,128)(2,1)}, u32[]{:S(2)}) copy-start(bf16[16,1024,64]{1,2,0:T(8,128)(2,1)} %param.13) | copy-start | bytes 6291460
  6.2 11.1 %copy-start.4 = (f32[64,16]{0,1:T(8,128)S(1)}, f32[64,16]{0,1:T(8,128)}, u32[]{:S(2)}) copy-start(f32[64,16]{0,1:T(8,128)} %param.14) | copy-start | bytes 12292
  6.2 11.1 %copy-start.5 = (f32[64]{0:T(128)S(1)}, f32[64]{0:T(128)}, u32[]{:S(2)}) copy-start(f32[64]{0:T(128)} %param.15) | copy-start | bytes 772
  9.0 16.5 %all-to-all-start = ((f32[32,1,1536]{2,1,0:T(1,128)}), f32[32,1,1536]{2,1,0:T(1,128)S(1)}, u32[]{:S(2)}, u32[]{:S(2)}) async-start(f32[32,1,1536]{2,1,0:T(1,128)} %bitcast), calls=%async_computation | async-start | bytes 393216 | tf_op jit(solution)/shard_map/all_to_all | solution.py:35
  25.5 11.4 %all-to-all-start.4 = ((bf16[32,2,512]{2,1,0:T(2,128)(2,1)}), bf16[32,2,512]{2,1,0:T(2,128)(2,1)S(1)}, u32[]{:S(2)}, u32[]{:S(2)}) async-start(bf16[32,2,512]{2,1,0:T(2,128)(2,1)} %reshape.64), calls=%async_computation.4 | async-start | bytes 131072 | tf_op jit(solution)/shard_map/all_to_all | solution.py:14
  37.6 12.0 %all-to-all-start.1 = ((f32[32,1,1536]{2,1,0:T(1,128)}), f32[32,1,1536]{2,1,0:T(1,128)S(1)}, u32[]{:S(2)}, u32[]{:S(2)}) async-start(f32[32,1,1536]{2,1,0:T(1,128)} %broadcast_in_dim.6), calls=%async_computation.1 | async-start | bytes 393216 | tf_op jit(solution)/shard_map/all_to_all | solution.py:14
  50.4 23.9 %all-to-all-start.5 = ((bf16[4,2048,16]{1,2,0:T(8,128)(2,1)}), bf16[4,2048,16]{1,2,0:T(8,128)(2,1)S(1)}, u32[]{:S(2)}, u32[]{:S(2)}) async-start(bf16[4,2048,16]{1,2,0:T(8,128)(2,1)} %broadcast_in_dim.15), calls=%async_computation.5 | async-start | bytes 524288 | tf_op jit(solution)/shard_map/all_to_all | solution.py:14
  74.2 39.6 %all-to-all-start.3 = ((bf16[32,2,16384]{2,1,0:T(2,128)(2,1)}), bf16[32,2,16384]{2,1,0:T(2,128)(2,1)S(1)}, u32[]{:S(2)}, u32[]{:S(2)}) async-start(bf16[32,2,16384]{2,1,0:T(2,128)(2,1)} %reshape.62), calls=%async_computation.3 | async-start | bytes 4194304 | tf_op jit(solution)/shard_map/all_to_all | solution.py:88
  113.9 61.3 %all-to-all-start.2 = ((bf16[32,2,32768]{2,1,0:T(2,128)(2,1)}), bf16[32,2,32768]{2,1,0:T(2,128)(2,1)}, u32[]{:S(2)}, u32[]{:S(2)}) async-start(bf16[32,2,32768]{2,1,0:T(2,128)(2,1)} %reshape.60), calls=%async_computation.2 | async-start | bytes 8388608 | tf_op jit(solution)/shard_map/all_to_all | solution.py:57
where the time goes:
time: 230 us; the launch traced here: 228 us
  local copies, waits for them, and re-layouts  118 us (51%)
  waiting for transfers between devices  57.5 us (25%)
  starting transfers between devices  32.4 us (14%)
  other arithmetic  19.7 us (9%)
    unnamed x23, local copies, waits for them, and re-layouts  43.1 us
    all_to_all x1, waiting for transfers between devices, in_one_piece(): lax.all_to_all(both, axis, split_axis=split_dim, concat_axis=concat_dim,...  35 us
    slice x5, local copies, waits for them, and re-layouts, in_one_piece(): outs.append(lax.slice_in_dim(filled, at, at + a.shape[along], axis=along))  28.7 us
    all_to_all x3, waiting for transfers between devices, from_everyone(): return lax.all_to_all(copies, axis, split_axis=0, concat_axis=0, tiled=True)  15.1 us
    all_to_all x2, local copies, waits for them, and re-layouts, shards(): lax.all_to_all(narrow_down, 'rows', split_axis=1, concat_axis=2, tiled=True)  13.6 us
    concatenate x1, local copies, waits for them, and re-layouts, in_one_piece(): both = jnp.concatenate(arrays, axis=along)  12.9 us
    all_to_all x3, starting transfers between devices, from_everyone(): return lax.all_to_all(copies, axis, split_axis=0, concat_axis=0, tiled=True)  12.6 us
    all_to_all x1, local copies, waits for them, and re-layouts, in_one_piece(): lax.all_to_all(both, axis, split_axis=split_dim, concat_axis=concat_dim,...  9.84 us
  transfers between devices with their start and end apart: 6, of which 4 were waited for; matrix products, arithmetic and copies ran while one was open for 30% of the time, Pallas kernels for 0%

commit v1 on v0

v1 whole, which is shorter than its diff:
```python
import functools

import jax
import jax.numpy as jnp
from jax import lax
from jax.experimental import pallas as pl
from jax.experimental.pallas import tpu as pltpu
from jax.sharding import PartitionSpec as P

MESH = pl.DeviceIdType.MESH
F32, BF16 = jnp.float32, jnp.bfloat16

SIDE = 4
CHIPS = 16
HALF = 8
JOBS = 24
BLOCKS = 8
PAIR = 2

GROUPS = ((0, 2, True), (2, 2, True), (4, 4, False), (8, 8, False), (16, 8, False))


def exchange(*refs):
    (w_gate, a_gate, w_up, a_up, w_down, a_down, r_weight, r_gain) = refs[:8]
    (o_gate, o_up, o_down, o_scale, o_router) = refs[8:13]
    (wide, narrow, ready, scale, inverse, all0, all1, part2, got2, sum2, part3, got3, sum3, part4, got4, sum4) = refs[13:29]
    (rw, rg, tile, load_sem, trade_out, trade_in, sum_out, sum_in, tot_in, ready_sem, done_sem, route_out, route_in, line_in, scale_sem) = refs[29:]
    weights, changes, outs = (w_gate, w_up, w_down), (a_gate, a_up, a_down), (o_gate, o_up, o_down)
    owner, row = lax.axis_index("owner"), lax.axis_index("rows")
    chip, core = row // 2, row % 2
    z, y = chip // SIDE, chip % SIDE
    other = 1 - core
    partner = (owner, chip * 2 + other)

    def chip_at(k):
        return (z + k // SIDE) % SIDE * SIDE + (y + k % SIDE) % SIDE

    def rows_of(which):
        return pl.ds(pl.multiple_of(which * 64, 64), 64)

    def loads(g):
        first, n, _ = GROUPS[g]
        m, e = first // HALF, first % HALF
        jobs = pl.ds(first, n)
        return [
            pltpu.make_async_copy(
                src.at[pl.ds(core * HALF + e, n)], dst.at[jobs, rows_of(core), :], load_sem.at[g, i]
            )
            for i, (src, dst) in enumerate(((weights[m], wide), (changes[m], narrow)))
        ]

    def trades(g):
        first, n, _ = GROUPS[g]
        m, e = first // HALF, first % HALF
        jobs = pl.ds(first, n)
        return [
            pltpu.make_async_remote_copy(
                src_ref=src.at[pl.ds(other * HALF + e, n)],
                dst_ref=dst.at[jobs, rows_of(core), :],
                send_sem=trade_out.at[g, i],
                recv_sem=trade_in.at[g, i],
                device_id=partner,
                device_id_type=MESH,
            )
            for i, (src, dst) in enumerate(((weights[m], wide), (changes[m], narrow)))
        ]

    route_local = [
        pltpu.make_async_copy(r_weight, rw.at[core], load_sem.at[len(GROUPS), 0]),
        pltpu.make_async_copy(r_gain, rg.at[core], load_sem.at[len(GROUPS), 1]),
    ]
    route_trade = [
        pltpu.make_async_remote_copy(
            src_ref=src, dst_ref=dst.at[core], send_sem=trade_out.at[len(GROUPS), i],
            recv_sem=trade_in.at[len(GROUPS), i], device_id=partner, device_id_type=MESH,
        )
        for i, (src, dst) in enumerate(((r_weight, rw), (r_gain, rg)))
    ]

    for g in range(len(GROUPS)):
        for copy in loads(g):
            copy.start()
    for copy in route_local:
        copy.start()

    barrier = pltpu.get_barrier_semaphore()
    pl.semaphore_signal(barrier, inc=1, device_id=partner, device_id_type=MESH)

    def greet(k, carry):
        for c in range(2):
            pl.semaphore_signal(
                barrier, inc=1, device_id=(owner, chip_at(k) * 2 + c), device_id_type=MESH
            )
        return carry

    lax.fori_loop(1, CHIPS, greet, 0)
    for k in range(1, SIDE):
        for c in range(2):
            pl.semaphore_signal(
                barrier, inc=1, device_id=((owner + k) % SIDE, chip * 2 + c), device_id_type=MESH
            )
    pl.semaphore_wait(barrier, 1 + 2 * (CHIPS - 1) + 2 * (SIDE - 1))

    for copy in trades(0) + trades(1) + route_trade:
        copy.start()
    for g in range(2, len(GROUPS)):
        for copy in trades(g):
            copy.start()

    def arrived(g):
        for copy in loads(g):
            copy.wait()
        for copy in trades(g):
            copy.wait_recv()

    def fresh(job, b):
        lanes = slice(b * 128, (b + 1) * 128)
        return wide[job, :, lanes] + narrow[job, :, lanes].astype(F32)

    def square_sum(job, b):
        x = fresh(job, b)
        return jnp.sum(x * x, axis=0, keepdims=True)

    def to_chips(src, dst, out_sem, in_sem):
        def go(k, carry):
            there = chip_at(k)
            pltpu.make_async_remote_copy(
                src_ref=src(there), dst_ref=dst, send_sem=out_sem, recv_sem=in_sem,
                device_id=(owner, there * 2 + core), device_id_type=MESH,
            ).start()
            return carry

        lax.fori_loop(1, CHIPS, go, 0)

    def wait_for(ref, sem):
        pltpu.make_async_copy(ref, ref, sem).wait()

    def keep(job, b, total):
        root = jnp.sqrt(total)
        scale[job, b] = root
        inverse[job, b] = 1.0 / root

    def sums_broadcast(g, got):
        first, n, _ = GROUPS[g]
        for i in range(n):
            for b in range(BLOCKS):
                got[chip, i, b : b + 1, :] = square_sum(first + i, b)
        to_chips(lambda there: got.at[chip], got.at[chip], sum_out.at[g], sum_in.at[g])

    def sums_added(g, got):
        first, n, _ = GROUPS[g]
        wait_for(got.at[pl.ds(0, CHIPS - 1)], sum_in.at[g])
        for i in range(n):
            total = got[0, i]
            for s in range(1, CHIPS):
                total = total + got[s, i]
            for b in range(BLOCKS):
                keep(first + i, b, total[b : b + 1, :])

    def sums_scattered(g, part, got):
        first, n, _ = GROUPS[g]
        per = n // 2

        def one(i, carry):
            for b in range(BLOCKS):
                line = i * BLOCKS + b
                part[line // per, line % per] = square_sum(first + i, b)
            return carry

        lax.fori_loop(0, n, one, 0)
        got[chip] = part[chip]
        to_chips(lambda there: part.at[there], got.at[chip], sum_out.at[g], sum_in.at[g])

    def sums_gathered(g, got, whole):
        wait_for(got.at[pl.ds(0, CHIPS - 1)], sum_in.at[g])
        total = got[0]
        for s in range(1, CHIPS):
            total = total + got[s]
        whole[chip] = total
        to_chips(lambda there: whole.at[chip], whole.at[chip], ready_sem.at[g], tot_in.at[g])

    def sums_taken(g, whole):
        first, n, _ = GROUPS[g]
        per = n // 2
        wait_for(whole.at[pl.ds(0, CHIPS - 1)], tot_in.at[g])

        def one(i, carry):
            for b in range(BLOCKS):
                line = i * BLOCKS + b
                keep(first + i, b, whole[line // per, line % per])
            return carry

        lax.fori_loop(0, n, one, 0)

    mine = pl.ds(pl.multiple_of(chip * 128, 128), 128)

    def send(out, at, job):
        for i in range(PAIR):

            def blocks(b, carry, i=i):
                lanes = pl.ds(pl.multiple_of(b * 128, 128), 128)
                x = wide[job + i, :, lanes] + narrow[job + i, :, lanes].astype(F32)
                x = x * inverse[job + i, b]
                ready[job + i, lanes, :] = x.T.astype(BF16)
                return carry

            lax.fori_loop(0, BLOCKS, blocks, 0)

        def go(k, carry):
            there = chip_at(CHIPS - k)
            for t in range(2):
                row_there = there * 2 + (core + t) % 2
                pltpu.make_async_remote_copy(
                    src_ref=ready.at[pl.ds(job, PAIR), pl.ds(pl.multiple_of(row_there * 32, 32), 32), :],
                    dst_ref=out.at[pl.ds(at, PAIR), :, mine],
                    send_sem=done_sem.at[0],
                    recv_sem=done_sem.at[1],
                    device_id=(owner, row_there),
                    device_id_type=MESH,
                ).start()
            return carry

        lax.fori_loop(1, CHIPS, go, 0)
        row_there = chip * 2 + other
        pltpu.make_async_remote_copy(
            src_ref=ready.at[pl.ds(job, PAIR), pl.ds(pl.multiple_of(row_there * 32, 32), 32), :],
            dst_ref=out.at[pl.ds(at, PAIR), :, mine],
            send_sem=done_sem.at[0],
            recv_sem=done_sem.at[1],
            device_id=partner,
            device_id_type=MESH,
        ).start()
        for i in range(PAIR):
            out[at + i, :, mine] = ready[job + i, pl.ds(pl.multiple_of(row * 32, 32), 32), :]

    def sends(first, n):
        m, e = first // HALF, first % HALF

        def one(i, carry):
            send(outs[m], core * HALF + e + i * PAIR, first + i * PAIR)
            return carry

        lax.fori_loop(0, n // PAIR, one, 0)

    def router_tile():
        for copy in route_local:
            copy.wait()
        for copy in route_trade:
            copy.wait_recv()
        folded = jnp.concatenate([rw[c] * rg[c] for c in range(2)], axis=1).astype(BF16)
        tile[...] = folded
        for_core = pl.ds(pl.multiple_of(core * HALF, HALF), HALF)
        lines = pl.ds(pl.multiple_of(owner * 16 + core * HALF, HALF), HALF)
        o_router[lines, mine] = jnp.where(core == 0, folded[:HALF], folded[HALF:])
        to_chips(lambda there: tile.at[for_core], o_router.at[lines, mine], route_out.at[0], route_in.at[0])

    lines = pl.ds(pl.multiple_of(owner * 16 + core * HALF, HALF), HALF)

    def router_lines():
        wait_for(o_router.at[pl.ds(0, HALF), pl.ds(0, 15 * 128)], route_in.at[0])
        for k in range(SIDE):
            for c in range(2):
                if k == 0 and c == 0:
                    continue
                to = ((owner + k) % SIDE, chip * 2 + (core + c) % 2)
                pltpu.make_async_remote_copy(
                    src_ref=o_router.at[lines, :], dst_ref=o_router.at[lines, :], send_sem=route_out.at[1],
                    recv_sem=line_in.at[0], device_id=to, device_id_type=MESH,
                ).start()

    arrived(0)
    sums_broadcast(0, all0)
    arrived(1)
    sums_broadcast(1, all1)
    router_tile()
    arrived(2)
    sums_scattered(2, part2, got2)
    sums_added(0, all0)
    sends(0, 2)
    sums_gathered(2, got2, sum2)
    sums_added(1, all1)
    sends(2, 2)
    arrived(3)
    sums_scattered(3, part3, got3)
    sums_taken(2, sum2)
    sends(4, 2)
    sums_gathered(3, got3, sum3)
    router_lines()
    sends(6, 2)
    arrived(4)
    sums_scattered(4, part4, got4)
    sums_taken(3, sum3)
    sends(8, 2)
    sums_gathered(4, got4, sum4)
    sends(10, 6)
    sums_taken(4, sum4)
    sends(16, 8)

    for b in range(1):
        o_scale[core] = scale[:, chip // 2]
        share = pltpu.make_async_remote_copy(
            src_ref=scale.at[:, chip // 2], dst_ref=o_scale.at[core], send_sem=scale_sem.at[0],
            recv_sem=scale_sem.at[1], device_id=partner, device_id_type=MESH,
        )
        share.start()

    for g, (first, n, _) in enumerate(GROUPS):
        for copy in trades(g):
            copy.wait_send()
    for copy in route_trade:
        copy.wait_send()
    for g, got in enumerate((all0, all1, got2, got3, got4)):
        wait_for(got.at[pl.ds(0, CHIPS - 1)], sum_out.at[g])
    for g, whole in ((2, sum2), (3, sum3), (4, sum4)):
        wait_for(whole.at[pl.ds(0, CHIPS - 1)], ready_sem.at[g])
    wait_for(o_router.at[pl.ds(0, HALF), pl.ds(0, 15 * 128)], route_out.at[0])
    for _ in range(7):
        wait_for(o_router.at[pl.ds(0, HALF), :], route_out.at[1])
    wait_for(o_router.at[pl.ds(0, 56), :], line_in.at[0])
    share.wait()
    for s in range(2):
        wait_for(ready.at[:, pl.ds(0, 31 * 32), :], done_sem.at[s])


def write_out(*refs):
    (gate, up, down, scale, router, o_gate, o_up, o_down, s_gate, s_up, s_down, o_router, sem) = refs
    copies = [
        pltpu.make_async_copy(src, dst, sem.at[i])
        for i, (src, dst) in enumerate(((gate, o_gate), (up, o_up), (down, o_down), (router, o_router)))
    ]
    for copy in copies:
        copy.start()
    row = lax.axis_index("rows")
    for m, out in enumerate((s_gate, s_up, s_down)):
        for c in range(2):
            block = scale[c, m * HALF : (m + 1) * HALF, 0, :]
            block = pltpu.roll(block, (128 - row % 4 * 32) % 128, 1)
            out[c * HALF : (c + 1) * HALF, :] = block[:, :32]
    for copy in copies:
        copy.wait()


def shards(w_gate, avg_gate, w_up, avg_up, w_down, avg_down, router_weight, router_gain):
    vmem, dma = pltpu.VMEM, pltpu.SemaphoreType.DMA
    hbm = pl.BlockSpec(memory_space=pltpu.HBM)
    anywhere = pl.BlockSpec(memory_space=pltpu.VMEM)
    served = (16, 32, 2048)
    gate, up, down, scale, router = pl.pallas_call(
        exchange,
        out_shape=[
            pltpu.VMEM(served, BF16), pltpu.VMEM(served, BF16), pltpu.VMEM(served, BF16),
            pltpu.VMEM((2, JOBS, 1, 128), F32), pltpu.VMEM((64, 2048), BF16),
        ],
        in_specs=[hbm] * 8,
        out_specs=[anywhere] * 5,
        scratch_shapes=[
            vmem((JOBS, 128, 1024), F32), vmem((JOBS, 128, 1024), BF16), vmem((JOBS, 1024, 128), BF16),
            vmem((JOBS, BLOCKS, 1, 128), F32), vmem((JOBS, BLOCKS, 1, 128), F32),
            vmem((CHIPS, 2, BLOCKS, 128), F32), vmem((CHIPS, 2, BLOCKS, 128), F32),
        ]
        + [vmem((CHIPS, n, 1, 128), F32) for n in (2, 2, 2, 4, 4, 4, 4, 4, 4)]
        + [
            vmem((2, 16, 64), F32), vmem((2, 1, 64), F32), vmem((16, 128), BF16),
            dma((6, 2)), dma((6, 2)), dma((6, 2)), dma((5,)), dma((5,)), dma((5,)), dma((5,)), dma((2,)),
            dma((2,)), dma((2,)), dma((1,)), dma((2,)),
        ],
        compiler_params=pltpu.CompilerParams(
            collective_id=0, has_side_effects=True, vmem_limit_bytes=48 << 20
        ),
        name="exchange",
    )(
        w_gate, avg_gate, w_up, avg_up, jnp.swapaxes(w_down, 1, 2), jnp.swapaxes(avg_down, 1, 2),
        router_weight.T, router_gain[None, :],
    )
    out = pl.BlockSpec(memory_space=pl.ANY)
    small = pl.BlockSpec(memory_space=pltpu.VMEM)
    gate, up, down, s_gate, s_up, s_down, router = pl.pallas_call(
        write_out,
        out_shape=[jax.ShapeDtypeStruct(served, BF16)] * 3
        + [jax.ShapeDtypeStruct((16, 32), F32)] * 3
        + [jax.ShapeDtypeStruct((64, 2048), BF16)],
        in_specs=[small] * 5,
        out_specs=[out] * 3 + [small] * 3 + [out],
        scratch_shapes=[dma((4,))],
        compiler_params=pltpu.CompilerParams(vmem_limit_bytes=8 << 20),
        name="write_out",
    )(*(pltpu.with_memory_space_constraint(x, pltpu.VMEM) for x in (gate, up, down, scale, router)))
    return (
        jnp.swapaxes(gate, 1, 2), jnp.swapaxes(up, 1, 2), down, s_gate, s_up, s_down, router.T,
    )


def solution(mesh):
    return jax.shard_map(
        shards,
        mesh=mesh,
        in_specs=(
            P("owner", "rows", None),
            P("owner", "rows", None),
            P("owner", "rows", None),
            P("owner", "rows", None),
            P("owner", None, "rows"),
            P("owner", None, "rows"),
            P("rows", "owner"),
            P("rows"),
        ),
        out_specs=(
            P("owner", None, "rows"),
            P("owner", None, "rows"),
            P("owner", "rows", None),
            P("owner", "rows"),
            P("owner", "rows"),
            P("owner", "rows"),
            P(),
        ),
        check_vma=False,
    )
```

time: 230 us -> 95.7 us (0.42)
  local copies, waits for them, and re-layouts: 118 us -> 0 us
  Pallas kernels: 0 us -> 93.7 us
  waiting for transfers between devices: 57.5 us -> 0 us
  starting transfers between devices: 32.4 us -> 0 us
  other arithmetic: 19.7 us -> 0 us
    pallas_call x0 -> x2, Pallas kernels: none -> 93.7 us  [the longest x1 90.3 us: shards(): pl.pallas_call(exchange, out_shape=[pltpu.VMEM(served, BF16), pltpu.VMEM(...]
    all_to_all x6 -> x0, waiting for transfers between devices: 57.5 us -> none  [the longest x1 35 us: in_one_piece(): lax.all_to_all(both, axis, split_axis=split_dim, concat_axis=concat_dim,...]
    unnamed x23 -> x0, local copies, waits for them, and re-layouts: 43.1 us -> none
    all_to_all x6 -> x0, starting transfers between devices: 32.4 us -> none  [the longest x3 12.6 us: from_everyone(): return lax.all_to_all(copies, axis, split_axis=0, concat_axis=0, tiled=True)]
    slice x6 -> x0, local copies, waits for them, and re-layouts: 28.8 us -> none  [the longest x5 28.7 us: in_one_piece(): outs.append(lax.slice_in_dim(filled, at, at + a.shape[along], axis=along))]
    all_to_all x4 -> x0, local copies, waits for them, and re-layouts: 23.5 us -> none  [the longest x2 13.6 us: shards(): lax.all_to_all(narrow_down, 'rows', split_axis=1, concat_axis=2, tiled=True)]
    concatenate x1 -> x0, local copies, waits for them, and re-layouts: 12.9 us -> none  [in_one_piece(): both = jnp.concatenate(arrays, axis=along)]
    convert_element_type x3 -> x0, other arithmetic: 10.7 us -> none  [the longest x1 6.29 us: shards(): (fresh_up / jnp.expand_dims(scale_up, 1)).astype(jnp.bfloat16)]
  transfers between devices with their start and end apart: 6 -> 0, of which waited for: 4 -> 0; matrix products, arithmetic and copies ran while one was open for 30% -> 0% of each run, Pallas kernels for 0% -> 0%
where the time goes in v1:
time: 95.7 us; the launch traced here: 94.3 us
  Pallas kernels  93.7 us (98%)
    pallas_call x1, Pallas kernels, shards(): pl.pallas_call(exchange, out_shape=[pltpu.VMEM(served, BF16), pltpu.VMEM(...  90.3 us
    pallas_call x1, Pallas kernels, shards(): pl.pallas_call(write_out, out_shape=[jax.ShapeDtypeStruct(served, BF16)]...  3.37 us

profile of v1, /device:TPU:2, one launch (start us, length us, event | category | flops | bytes accessed | tf_op | source)
XLA Modules:
  0.0 94.3 jit_solution(3703626024315713966)
XLA Ops:
  0.6 90.3 %exchange.1 = (bf16[16,32,2048]{2,1,0:T(8,128)(2,1)S(1)}, bf16[16,32,2048]{2,1,0:T(8,128)(2,1)S(1)}, bf16[16,32,2048]{2,1,0:T(8,128)(2,1)S(1)}, f32[2,24,1,128]{3,2,1,0:T(1,128)S(1)}, bf16[64,2048]{1,0:T(8,128)(2,1)S(1)}) custom-call(f32[16,64,1024]{2,1,0:T(8,128)} %refs_0_.1, bf16[16,64,1024]{2,1,0:T(8,128)(2,1)} %refs_1_.1, f32[16,64,1024]{2,1,0:T(8,128)} %refs_2_.1, ...), custom_call_target="tpu_custom_call" | custom-call | tf_op jit(solution)/shard_map/exchange/pallas_call | solution.py:348
  90.9 3.4 %write_out.1 = (bf16[16,32,2048]{2,1,0:T(8,128)(2,1)}, bf16[16,32,2048]{2,1,0:T(8,128)(2,1)}, bf16[16,32,2048]{2,1,0:T(8,128)(2,1)}, f32[16,32]{1,0:T(8,128)}, f...) custom-call(bf16[16,32,2048]{2,1,0:T(8,128)(2,1)S(1)} %get-tuple-element.19.refs_0_, ...), custom_call_target="tpu_custom_call" | custom-call | tf_op jit(solution)/shard_map/write_out/pallas_call | solution.py:377

commit v2 on v1

v2 whole, which is shorter than its diff:
```python
import jax
import jax.numpy as jnp
from jax import lax
from jax.experimental import pallas as pl
from jax.experimental.pallas import tpu as pltpu
from jax.sharding import PartitionSpec as P

MESH = pl.DeviceIdType.MESH
F32, BF16 = jnp.float32, jnp.bfloat16

SIDE = 4
CHIPS = 16
HALF = 8
JOBS = 24
BLOCKS = 8

LOADS = ((0, 2), (2, 2), (4, 4), (8, 8), (16, 8))
SUMS = ((0, 2), (2, 2), (4, 4), (8, 16))


def exchange(*refs):
    (w_gate, a_gate, w_up, a_up, w_down, a_down, r_weight, r_gain) = refs[:8]
    (o_gate, o_up, o_down, o_scale, o_router) = refs[8:13]
    (wide, narrow, ready, scale, inverse, near_w, near_a, kept, given, taken) = refs[13:23]
    (all0, all1, part2, got2, sum2, part3, got3, sum3) = refs[23:31]
    (rw, rg, tile, load_sem, near_sem, trade_out, trade_in, sum_out, sum_in, ready_sem, tot_in,
     done_sem, route_sem, line_sem, scale_sem, near_share) = refs[31:]
    weights, changes, outs = (w_gate, w_up, w_down), (a_gate, a_up, a_down), (o_gate, o_up, o_down)
    owner, row = lax.axis_index("owner"), lax.axis_index("rows")
    chip, core = row // 2, row % 2
    z, y = chip // SIDE, chip % SIDE
    other = 1 - core
    partner_row = chip * 2 + other
    partner = (owner, partner_row)

    def chip_at(k):
        return (z + k // SIDE) % SIDE * SIDE + (y + k % SIDE) % SIDE

    def rows_of(which):
        return pl.ds(pl.multiple_of(which * 64, 64), 64)

    def to_partner(src, dst, out_sem, in_sem):
        return pltpu.make_async_remote_copy(
            src_ref=src, dst_ref=dst, send_sem=out_sem, recv_sem=in_sem, device_id=partner,
            device_id_type=MESH,
        )

    def sources(g):
        first, n = LOADS[g]
        m, e = first // HALF, first % HALF
        return first, n, e, ((weights[m], wide), (changes[m], narrow))

    def loads(g):
        first, n, e, pairs = sources(g)
        return [
            pltpu.make_async_copy(
                src.at[pl.ds(core * HALF + e, n)], dst.at[pl.ds(first, n), rows_of(core), :], load_sem.at[g, i]
            )
            for i, (src, dst) in enumerate(pairs)
        ]

    def near_loads(g):
        first, n, e, pairs = sources(g)
        return [
            pltpu.make_async_copy(
                src.at[pl.ds(other * HALF + e, n)], dst.at[pl.ds(first, n)], near_sem.at[g, i]
            )
            for i, ((src, _), dst) in enumerate(zip(pairs, (near_w, near_a)))
        ]

    def trades(g):
        first, n, e, pairs = sources(g)
        return [
            to_partner(
                src.at[pl.ds(other * HALF + e, n)], dst.at[pl.ds(first, n), rows_of(core), :],
                trade_out.at[g, i], trade_in.at[g, i],
            )
            for i, (src, dst) in enumerate(pairs)
        ]

    last = len(LOADS)
    route_local = [
        pltpu.make_async_copy(src, dst.at[core], load_sem.at[last, i])
        for i, (src, dst) in enumerate(((r_weight, rw), (r_gain, rg)))
    ]
    route_trade = [
        to_partner(src, dst.at[core], trade_out.at[last, i], trade_in.at[last, i])
        for i, (src, dst) in enumerate(((r_weight, rw), (r_gain, rg)))
    ]

    for g in range(3):
        for copy in loads(g) + near_loads(g):
            copy.start()
    for copy in route_local:
        copy.start()
    for g in (3, 4):
        for copy in loads(g) + near_loads(g):
            copy.start()

    barrier = pltpu.get_barrier_semaphore()

    def greet(k, carry):
        for c in range(2):
            pl.semaphore_signal(
                barrier, inc=1, device_id=(owner, chip_at(CHIPS - k) * 2 + c), device_id_type=MESH
            )
        return carry

    lax.fori_loop(1, CHIPS, greet, 0)
    for k in range(1, SIDE):
        for c in range(2):
            pl.semaphore_signal(
                barrier, inc=1, device_id=((owner + k) % SIDE, chip * 2 + c), device_id_type=MESH
            )
    pl.semaphore_signal(barrier, inc=1, device_id=partner, device_id_type=MESH)

    def lanes_of(b):
        return slice(b * 128, (b + 1) * 128)

    def squares(x):
        return jnp.sum(x * x, axis=0, keepdims=True)

    def own_rows(g):
        first, n = LOADS[g]
        for copy in loads(g) + near_loads(g):
            copy.wait()

        def one(job, carry):
            for b in range(BLOCKS):
                lanes = lanes_of(b)
                given[job, b : b + 1, :] = squares(near_w[job, :, lanes] + near_a[job, :, lanes].astype(F32))
                kept[job, b : b + 1, :] = squares(
                    wide[job, rows_of(core), lanes] + narrow[job, rows_of(core), lanes].astype(F32)
                )
            return carry

        lax.fori_loop(first, first + n, one, 0)

    def shared(k, first, n):
        jobs = pl.ds(first, n)
        return to_partner(given.at[jobs], taken.at[jobs], near_share.at[k, 0], near_share.at[k, 1])

    near = [shared(0, 0, 8), shared(1, 8, 16)]
    for g in range(3):
        own_rows(g)

    pl.semaphore_wait(barrier, 1 + 2 * (CHIPS - 1) + 2 * (SIDE - 1))

    near[0].start()
    for copy in route_trade + trades(0) + trades(1):
        copy.start()

    def traded(g):
        for copy in trades(g):
            copy.wait_recv()

    def to_chips(src, dst, out_sem, in_sem):
        def go(k, carry):
            there = chip_at(k)
            pltpu.make_async_remote_copy(
                src_ref=src(there), dst_ref=dst, send_sem=out_sem, recv_sem=in_sem,
                device_id=(owner, there * 2 + core), device_id_type=MESH,
            ).start()
            return carry

        lax.fori_loop(1, CHIPS, go, 0)

    def wait_for(ref, sem):
        pltpu.make_async_copy(ref, ref, sem).wait()

    def keep(job, b, total):
        root = jnp.sqrt(total)
        scale[job, b] = root
        inverse[job, b] = 1.0 / root

    def sums_broadcast(g, got):
        first, n = SUMS[g]
        for i in range(n):
            got[chip, i] = kept[first + i] + taken[first + i]
        to_chips(lambda there: got.at[chip], got.at[chip], sum_out.at[g], sum_in.at[g])

    def sums_added(g, got):
        first, n = SUMS[g]
        wait_for(got.at[pl.ds(0, CHIPS - 1)], sum_in.at[g])
        for i in range(n):
            total = got[0, i]
            for s in range(1, CHIPS):
                total = total + got[s, i]
            for b in range(BLOCKS):
                keep(first + i, b, total[b : b + 1, :])

    def sums_scattered(g, part, got):
        first, n = SUMS[g]
        per = n // 2

        def one(i, carry):
            total = kept[first + i] + taken[first + i]
            if n == CHIPS:
                part[i] = total
                return carry
            for b in range(BLOCKS):
                line = i * BLOCKS + b
                part[line // per, line % per] = total[b : b + 1, :]
            return carry

        lax.fori_loop(0, n, one, 0)
        got[chip] = part[chip]
        to_chips(lambda there: part.at[there], got.at[chip], sum_out.at[g], sum_in.at[g])

    def sums_gathered(g, got, whole):
        wait_for(got.at[pl.ds(0, CHIPS - 1)], sum_in.at[g])
        total = got[0]
        for s in range(1, CHIPS):
            total = total + got[s]
        whole[chip] = total
        to_chips(lambda there: whole.at[chip], whole.at[chip], ready_sem.at[g], tot_in.at[g])

    def sums_taken(g, whole):
        first, n = SUMS[g]
        per = n // 2
        wait_for(whole.at[pl.ds(0, CHIPS - 1)], tot_in.at[g])

        def one(i, carry):
            for b in range(BLOCKS):
                line = i * BLOCKS + b
                keep(first + i, b, whole[i, b : b + 1, :] if n == CHIPS else whole[line // per, line % per])
            return carry

        lax.fori_loop(0, n, one, 0)

    mine = pl.ds(pl.multiple_of(chip * 128, 128), 128)

    def lines_for(which):
        return pl.ds(pl.multiple_of(which * 32, 32), 32)

    def to_all(send):
        def go(k, carry):
            there = chip_at(CHIPS - k)
            for t in range(2):
                send(there * 2 + (core + t) % 2)
            return carry

        lax.fori_loop(1, CHIPS, go, 0)
        send(partner_row)

    def normalise(job):
        def blocks(b, carry):
            lanes = pl.ds(pl.multiple_of(b * 128, 128), 128)
            x = wide[job, :, lanes] + narrow[job, :, lanes].astype(F32)
            ready[job, lanes, :] = (x * inverse[job, b]).astype(BF16).T
            return carry

        lax.fori_loop(0, BLOCKS, blocks, 0)

    def issue(m, job):
        at = core * HALF + job - m * HALF

        def send(to):
            pltpu.make_async_remote_copy(
                src_ref=ready.at[job, lines_for(to), :], dst_ref=outs[m].at[at, :, mine],
                send_sem=done_sem.at[0], recv_sem=done_sem.at[1], device_id=(owner, to), device_id_type=MESH,
            ).start()

        to_all(send)
        outs[m][at, :, mine] = ready[job, lines_for(row), :]

    def sends(m, first, n):
        def one(i, carry):
            normalise(first + i)
            issue(m, first + i)
            return carry

        lax.fori_loop(0, n, one, 0)

    lines = pl.ds(pl.multiple_of(owner * 16 + core * HALF, HALF), HALF)

    def router_tile():
        for copy in route_local:
            copy.wait()
        for copy in route_trade:
            copy.wait_recv()
        folded = jnp.concatenate([rw[c] * rg[c] for c in range(2)], axis=1).astype(BF16)
        tile[...] = folded
        for_core = pl.ds(pl.multiple_of(core * HALF, HALF), HALF)
        o_router[lines, mine] = jnp.where(core == 0, folded[:HALF], folded[HALF:])
        to_chips(lambda there: tile.at[for_core], o_router.at[lines, mine], route_sem.at[0], route_sem.at[1])

    def router_lines():
        wait_for(o_router.at[pl.ds(0, HALF), pl.ds(0, 15 * 128)], route_sem.at[1])
        for k in range(SIDE):
            for c in range(2):
                if k == 0 and c == 0:
                    continue
                to = ((owner + k) % SIDE, chip * 2 + (core + c) % 2)
                pltpu.make_async_remote_copy(
                    src_ref=o_router.at[lines, :], dst_ref=o_router.at[lines, :], send_sem=line_sem.at[0],
                    recv_sem=line_sem.at[1], device_id=to, device_id_type=MESH,
                ).start()

    near[0].wait_recv()
    sums_broadcast(0, all0)
    sums_scattered(2, part2, got2)
    sums_broadcast(1, all1)
    own_rows(3)
    own_rows(4)
    near[1].start()
    for copy in trades(2) + trades(3) + trades(4):
        copy.start()
    near[1].wait_recv()
    sums_scattered(3, part3, got3)
    traded(0)
    sums_added(0, all0)
    sends(0, 0, 1)
    sums_gathered(2, got2, sum2)
    sends(0, 1, 1)
    router_tile()
    sums_added(1, all1)
    traded(1)
    sends(0, 2, 1)
    normalise(3)
    sums_gathered(3, got3, sum3)
    issue(0, 3)
    router_lines()
    traded(2)
    sums_taken(2, sum2)
    sends(0, 4, 4)
    traded(3)
    sums_taken(3, sum3)
    sends(1, 8, 8)
    traded(4)
    sends(2, 16, 8)

    o_scale[core] = scale[:, chip // 2]
    share = to_partner(scale.at[:, chip // 2], o_scale.at[core], scale_sem.at[0], scale_sem.at[1])
    share.start()

    for copy in near:
        copy.wait_send()
    for g in range(len(LOADS)):
        for copy in trades(g):
            copy.wait_send()
    for copy in route_trade:
        copy.wait_send()
    for g, got in enumerate((all0, all1, got2, got3)):
        wait_for(got.at[pl.ds(0, CHIPS - 1)], sum_out.at[g])
    for g, whole in ((2, sum2), (3, sum3)):
        wait_for(whole.at[pl.ds(0, CHIPS - 1)], ready_sem.at[g])
    wait_for(o_router.at[pl.ds(0, HALF), pl.ds(0, 15 * 128)], route_sem.at[0])
    for s in range(2):
        wait_for(o_router.at[pl.ds(0, 56), :], line_sem.at[s])
    share.wait()
    for s in range(2):
        wait_for(ready.at[:, pl.ds(0, 31 * 32), :], done_sem.at[s])


def write_out(*refs):
    (gate, up, down, scale, router, o_gate, o_up, o_down, *rest) = refs
    (*o_scales, o_router, lines, sem) = rest
    large = [
        pltpu.make_async_copy(src, dst, sem.at[i])
        for i, (src, dst) in enumerate(((gate, o_gate), (up, o_up), (down, o_down), (router, o_router)))
    ]
    for copy in large:
        copy.start()
    row = lax.axis_index("rows")
    for m in range(3):
        for c in range(2):
            block = scale[c, m * HALF : (m + 1) * HALF, 0, :]
            block = pltpu.roll(block, (128 - row % 4 * 32) % 128, 1)
            lines[m, c * HALF : (c + 1) * HALF, :] = block[:, :32]
    small = [pltpu.make_async_copy(lines.at[m], out, sem.at[4 + m]) for m, out in enumerate(o_scales)]
    for copy in small:
        copy.start()
    for copy in large + small:
        copy.wait()


def shards(w_gate, avg_gate, w_up, avg_up, w_down, avg_down, router_weight, router_gain):
    vmem, dma = pltpu.VMEM, pltpu.SemaphoreType.DMA
    hbm = pl.BlockSpec(memory_space=pltpu.HBM)
    inside = pl.BlockSpec(memory_space=pltpu.VMEM)
    served = (16, 32, 2048)
    found = pl.pallas_call(
        exchange,
        out_shape=[vmem(served, BF16)] * 3
        + [vmem((2, JOBS, 1, 128), F32), vmem((64, 2048), BF16)],
        in_specs=[hbm] * 8,
        out_specs=[inside] * 5,
        scratch_shapes=[
            vmem((JOBS, 128, 1024), F32), vmem((JOBS, 128, 1024), BF16), vmem((JOBS, 1024, 128), BF16),
            vmem((JOBS, BLOCKS, 1, 128), F32), vmem((JOBS, BLOCKS, 1, 128), F32),
            vmem((JOBS, 64, 1024), F32), vmem((JOBS, 64, 1024), BF16),
        ]
        + [vmem((JOBS, BLOCKS, 128), F32)] * 3
        + [
            vmem((CHIPS, 2, BLOCKS, 128), F32), vmem((CHIPS, 2, BLOCKS, 128), F32),
        ]
        + [vmem((CHIPS, 2, 1, 128), F32)] * 3
        + [vmem((CHIPS, BLOCKS, 128), F32)] * 3
        + [
            vmem((2, 16, 64), F32), vmem((2, 1, 64), F32), vmem((16, 128), BF16),
            dma((6, 2)), dma((5, 2)), dma((6, 2)), dma((6, 2)), dma((4,)), dma((4,)), dma((4,)),
            dma((4,)), dma((2,)), dma((2,)), dma((2,)), dma((2,)), dma((2, 2)),
        ],
        compiler_params=pltpu.CompilerParams(
            collective_id=0, has_side_effects=True, vmem_limit_bytes=48 << 20
        ),
        name="exchange",
    )(
        w_gate, avg_gate, w_up, avg_up, jnp.swapaxes(w_down, 1, 2), jnp.swapaxes(avg_down, 1, 2),
        router_weight.T, router_gain[None, :],
    )
    out = pl.BlockSpec(memory_space=pl.ANY)
    gate, up, down, s_gate, s_up, s_down, router = pl.pallas_call(
        write_out,
        out_shape=[jax.ShapeDtypeStruct(served, BF16)] * 3
        + [jax.ShapeDtypeStruct((16, 32), F32)] * 3
        + [jax.ShapeDtypeStruct((64, 2048), BF16)],
        in_specs=[inside] * 5,
        out_specs=[out] * 7,
        scratch_shapes=[vmem((3, 16, 32), F32), dma((7,))],
        compiler_params=pltpu.CompilerParams(vmem_limit_bytes=8 << 20),
        name="write_out",
    )(*(pltpu.with_memory_space_constraint(x, pltpu.VMEM) for x in found))
    return (
        jnp.swapaxes(gate, 1, 2), jnp.swapaxes(up, 1, 2), down, s_gate, s_up, s_down, router.T,
    )


def solution(mesh):
    return jax.shard_map(
        shards,
        mesh=mesh,
        in_specs=(
            P("owner", "rows", None),
            P("owner", "rows", None),
            P("owner", "rows", None),
            P("owner", "rows", None),
            P("owner", None, "rows"),
            P("owner", None, "rows"),
            P("rows", "owner"),
            P("rows"),
        ),
        out_specs=(
            P("owner", None, "rows"),
            P("owner", None, "rows"),
            P("owner", "rows", None),
            P("owner", "rows"),
            P("owner", "rows"),
            P("owner", "rows"),
            P(),
        ),
        check_vma=False,
    )
```

time: 95.7 us -> 90.9 us (0.950)
  Pallas kernels: 93.7 us -> 89.1 us
    pallas_call x1, Pallas kernels: 90.3 us -> 86.3 us  [shards(): pl.pallas_call(exchange, out_shape=[vmem(served, BF16)] * 3 + [vmem((2, J...]
where the time goes in v2:
time: 90.9 us; the launch traced here: 89.7 us
  Pallas kernels  89.1 us (98%)
    pallas_call x1, Pallas kernels, shards(): pl.pallas_call(exchange, out_shape=[vmem(served, BF16)] * 3 + [vmem((2, J...  86.3 us
    pallas_call x1, Pallas kernels, shards(): pl.pallas_call(write_out, out_shape=[jax.ShapeDtypeStruct(served, BF16)]...  2.8 us

profile of v2, /device:TPU:2, one launch (start us, length us, event | category | flops | bytes accessed | tf_op | source)
XLA Modules:
  0.0 89.7 jit_solution(10618172689619605661)
XLA Ops:
  0.6 86.3 %exchange.1 = (bf16[16,32,2048]{2,1,0:T(8,128)(2,1)S(1)}, bf16[16,32,2048]{2,1,0:T(8,128)(2,1)S(1)}, bf16[16,32,2048]{2,1,0:T(8,128)(2,1)S(1)}, f32[2,24,1,128]{3,2,1,0:T(1,128)S(1)}, bf16[64,2048]{1,0:T(8,128)(2,1)S(1)}) custom-call(f32[16,64,1024]{2,1,0:T(8,128)} %refs_0_.1, bf16[16,64,1024]{2,1,0:T(8,128)(2,1)} %refs_1_.1, f32[16,64,1024]{2,1,0:T(8,128)} %refs_2_.1, ...), custom_call_target="tpu_custom_call" | custom-call | tf_op jit(solution)/shard_map/exchange/pallas_call | solution.py:383
  86.9 2.8 %write_out.1 = (bf16[16,32,2048]{2,1,0:T(8,128)(2,1)}, bf16[16,32,2048]{2,1,0:T(8,128)(2,1)}, bf16[16,32,2048]{2,1,0:T(8,128)(2,1)}, f32[16,32]{1,0:T(8,128)}, f...) custom-call(bf16[16,32,2048]{2,1,0:T(8,128)(2,1)S(1)} %get-tuple-element.19.refs_0_, ...), custom_call_target="tpu_custom_call" | custom-call | tf_op jit(solution)/shard_map/write_out/pallas_call | solution.py:414

commit v3 on v2

--- a/solution.py
+++ b/solution.py
@@ -14,8 +14,9 @@
 JOBS = 24
 BLOCKS = 8
 
-LOADS = ((0, 2), (2, 2), (4, 4), (8, 8), (16, 8))
-SUMS = ((0, 2), (2, 2), (4, 4), (8, 16))
+ORDER = (10, 1, 4, 3, 12, 6, 9, 5, 15, 14, 11, 7, 13, 2, 8)
+LOADS = ((0, 1), (1, 3), (4, 4), (8, 8), (16, 8))
+SUMS = ((0, 1), (1, 3), (4, 4), (8, 16))
 
 
 def exchange(*refs):
@@ -88,14 +89,8 @@
         for i, (src, dst) in enumerate(((r_weight, rw), (r_gain, rg)))
     ]
 
-    for g in range(3):
-        for copy in loads(g) + near_loads(g):
-            copy.start()
-    for copy in route_local:
-        copy.start()
-    for g in (3, 4):
-        for copy in loads(g) + near_loads(g):
-            copy.start()
+    for copy in loads(0) + near_loads(0):
+        copy.start()
 
     barrier = pltpu.get_barrier_semaphore()
 
@@ -114,6 +109,12 @@
             )
     pl.semaphore_signal(barrier, inc=1, device_id=partner, device_id_type=MESH)
 
+    for g in range(1, len(LOADS)):
+        for copy in loads(g) + near_loads(g):
+            copy.start()
+    for copy in route_local:
+        copy.start()
+
     def lanes_of(b):
         return slice(b * 128, (b + 1) * 128)
 
@@ -140,15 +141,10 @@
         jobs = pl.ds(first, n)
         return to_partner(given.at[jobs], taken.at[jobs], near_share.at[k, 0], near_share.at[k, 1])
 
-    near = [shared(0, 0, 8), shared(1, 8, 16)]
-    for g in range(3):
-        own_rows(g)
+    near = [shared(0, 1, 3), shared(1, 4, 4), shared(2, 8, 16)]
+    own_rows(0)
 
     pl.semaphore_wait(barrier, 1 + 2 * (CHIPS - 1) + 2 * (SIDE - 1))
-
-    near[0].start()
-    for copy in route_trade + trades(0) + trades(1):
-        copy.start()
 
     def traded(g):
         for copy in trades(g):
@@ -172,6 +168,31 @@
         root = jnp.sqrt(total)
         scale[job, b] = root
         inverse[job, b] = 1.0 / root
+
+    def sums_from_all(g, got):
+        def send(src, to):
+            pltpu.make_async_remote_copy(
+                src_ref=src.at[0], dst_ref=got.at[row], send_sem=sum_out.at[g], recv_sem=sum_in.at[g],
+                device_id=(owner, to), device_id_type=MESH,
+            ).start()
+
+        def go(k, carry):
+            there = chip_at(CHIPS - k)
+            send(kept, there * 2 + core)
+            send(given, there * 2 + other)
+            return carry
+
+        lax.fori_loop(1, CHIPS, go, 0)
+        send(given, partner_row)
+        got[row] = kept[0]
+
+    def sums_from_all_added(g, got):
+        wait_for(got.at[pl.ds(0, 2 * CHIPS - 1)], sum_in.at[g])
+        total = got[0]
+        for s in range(1, 2 * CHIPS):
+            total = total + got[s]
+        for b in range(BLOCKS):
+            keep(0, b, total[b : b + 1, :])
 
     def sums_broadcast(g, got):
         first, n = SUMS[g]
@@ -234,13 +255,10 @@
         return pl.ds(pl.multiple_of(which * 32, 32), 32)
 
     def to_all(send):
-        def go(k, carry):
-            there = chip_at(CHIPS - k)
+        for k in ORDER:
+            there = chip_at(k)
             for t in range(2):
                 send(there * 2 + (core + t) % 2)
-            return carry
-
-        lax.fori_loop(1, CHIPS, go, 0)
         send(partner_row)
 
     def normalise(job):
@@ -297,36 +315,46 @@
                     recv_sem=line_sem.at[1], device_id=to, device_id_type=MESH,
                 ).start()
 
+    sums_from_all(0, all0)
+    own_rows(1)
+    near[0].start()
+    for copy in trades(0) + route_trade:
+        copy.start()
+    own_rows(2)
+    near[1].start()
+    for copy in trades(1):
+        copy.start()
     near[0].wait_recv()
-    sums_broadcast(0, all0)
+    sums_broadcast(1, all1)
+    near[1].wait_recv()
     sums_scattered(2, part2, got2)
-    sums_broadcast(1, all1)
     own_rows(3)
     own_rows(4)
-    near[1].start()
+    near[2].start()
     for copy in trades(2) + trades(3) + trades(4):
         copy.start()
-    near[1].wait_recv()
+    traded(0)
+    sums_from_all_added(0, all0)
+    sends(0, 0, 1)
+    near[2].wait_recv()
     sums_scattered(3, part3, got3)
-    traded(0)
-    sums_added(0, all0)
-    sends(0, 0, 1)
+    traded(1)
+    sums_added(1, all1)
+    normalise(1)
     sums_gathered(2, got2, sum2)
-    sends(0, 1, 1)
+    issue(0, 1)
+    sends(0, 2, 2)
     router_tile()
-    sums_added(1, all1)
-    traded(1)
-    sends(0, 2, 1)
-    normalise(3)
-    sums_gathered(3, got3, sum3)
-    issue(0, 3)
-    router_lines()
     traded(2)
     sums_taken(2, sum2)
-    sends(0, 4, 4)
+    normalise(4)
+    sums_gathered(3, got3, sum3)
+    issue(0, 4)
+    sends(0, 5, 3)
     traded(3)
     sums_taken(3, sum3)
     sends(1, 8, 8)
+    router_lines()
     traded(4)
     sends(2, 16, 8)
 
@@ -342,7 +370,7 @@
     for copy in route_trade:
         copy.wait_send()
     for g, got in enumerate((all0, all1, got2, got3)):
-        wait_for(got.at[pl.ds(0, CHIPS - 1)], sum_out.at[g])
+        wait_for(got.at[pl.ds(0, got.shape[0] - 1)], sum_out.at[g])
     for g, whole in ((2, sum2), (3, sum3)):
         wait_for(whole.at[pl.ds(0, CHIPS - 1)], ready_sem.at[g])
     wait_for(o_router.at[pl.ds(0, HALF), pl.ds(0, 15 * 128)], route_sem.at[0])
@@ -393,14 +421,14 @@
         ]
         + [vmem((JOBS, BLOCKS, 128), F32)] * 3
         + [
-            vmem((CHIPS, 2, BLOCKS, 128), F32), vmem((CHIPS, 2, BLOCKS, 128), F32),
+            vmem((2 * CHIPS, BLOCKS, 128), F32), vmem((CHIPS, 3, BLOCKS, 128), F32),
         ]
         + [vmem((CHIPS, 2, 1, 128), F32)] * 3
         + [vmem((CHIPS, BLOCKS, 128), F32)] * 3
         + [
             vmem((2, 16, 64), F32), vmem((2, 1, 64), F32), vmem((16, 128), BF16),
             dma((6, 2)), dma((5, 2)), dma((6, 2)), dma((6, 2)), dma((4,)), dma((4,)), dma((4,)),
-            dma((4,)), dma((2,)), dma((2,)), dma((2,)), dma((2,)), dma((2, 2)),
+            dma((4,)), dma((2,)), dma((2,)), dma((2,)), dma((2,)), dma((3, 2)),
         ],
         compiler_params=pltpu.CompilerParams(
             collective_id=0, has_side_effects=True, vmem_limit_bytes=48 << 20

time: 90.9 us -> 90.3 us (level)
  no operation moved by 1% of the time
where the time goes in v3:
time: 90.3 us; the launch traced here: 89.1 us
  Pallas kernels  88.4 us (98%)
    pallas_call x1, Pallas kernels, shards(): pl.pallas_call(exchange, out_shape=[vmem(served, BF16)] * 3 + [vmem((2, J...  85.6 us
    pallas_call x1, Pallas kernels, shards(): pl.pallas_call(write_out, out_shape=[jax.ShapeDtypeStruct(served, BF16)]...  2.8 us

profile of v3, /device:TPU:2, one launch (start us, length us, event | category | flops | bytes accessed | tf_op | source)
XLA Modules:
  0.0 89.1 jit_solution(14519166631077165951)
XLA Ops:
  0.6 85.6 %exchange.1 = (bf16[16,32,2048]{2,1,0:T(8,128)(2,1)S(1)}, bf16[16,32,2048]{2,1,0:T(8,128)(2,1)S(1)}, bf16[16,32,2048]{2,1,0:T(8,128)(2,1)S(1)}, f32[2,24,1,128]{3,2,1,0:T(1,128)S(1)}, bf16[64,2048]{1,0:T(8,128)(2,1)S(1)}) custom-call(f32[16,64,1024]{2,1,0:T(8,128)} %refs_0_.1, bf16[16,64,1024]{2,1,0:T(8,128)(2,1)} %refs_1_.1, f32[16,64,1024]{2,1,0:T(8,128)} %refs_2_.1, ...), custom_call_target="tpu_custom_call" | custom-call | tf_op jit(solution)/shard_map/exchange/pallas_call | solution.py:411
  86.3 2.8 %write_out.1 = (bf16[16,32,2048]{2,1,0:T(8,128)(2,1)}, bf16[16,32,2048]{2,1,0:T(8,128)(2,1)}, bf16[16,32,2048]{2,1,0:T(8,128)(2,1)}, f32[16,32]{1,0:T(8,128)}, f...) custom-call(bf16[16,32,2048]{2,1,0:T(8,128)(2,1)S(1)} %get-tuple-element.19.refs_0_, ...), custom_call_target="tpu_custom_call" | custom-call | tf_op jit(solution)/shard_map/write_out/pallas_call | solution.py:442

commit v4 on v3

--- a/solution.py
+++ b/solution.py
@@ -15,6 +15,8 @@
 BLOCKS = 8
 
 ORDER = (10, 1, 4, 3, 12, 6, 9, 5, 15, 14, 11, 7, 13, 2, 8)
+FAR = (10, 14, 11, 6, 9, 8, 2, 13, 7, 15, 5, 12, 3, 4, 1)
+
 LOADS = ((0, 1), (1, 3), (4, 4), (8, 8), (16, 8))
 SUMS = ((0, 1), (1, 3), (4, 4), (8, 16))
 
@@ -94,14 +96,11 @@
 
     barrier = pltpu.get_barrier_semaphore()
 
-    def greet(k, carry):
+    for k in FAR:
         for c in range(2):
             pl.semaphore_signal(
-                barrier, inc=1, device_id=(owner, chip_at(CHIPS - k) * 2 + c), device_id_type=MESH
+                barrier, inc=1, device_id=(owner, chip_at(k) * 2 + c), device_id_type=MESH
             )
-        return carry
-
-    lax.fori_loop(1, CHIPS, greet, 0)
     for k in range(1, SIDE):
         for c in range(2):
             pl.semaphore_signal(
@@ -151,15 +150,12 @@
             copy.wait_recv()
 
     def to_chips(src, dst, out_sem, in_sem):
-        def go(k, carry):
+        for k in FAR:
             there = chip_at(k)
             pltpu.make_async_remote_copy(
                 src_ref=src(there), dst_ref=dst, send_sem=out_sem, recv_sem=in_sem,
                 device_id=(owner, there * 2 + core), device_id_type=MESH,
             ).start()
-            return carry
-
-        lax.fori_loop(1, CHIPS, go, 0)
 
     def wait_for(ref, sem):
         pltpu.make_async_copy(ref, ref, sem).wait()
@@ -176,13 +172,10 @@
                 device_id=(owner, to), device_id_type=MESH,
             ).start()
 
-        def go(k, carry):
-            there = chip_at(CHIPS - k)
+        for k in FAR:
+            there = chip_at(k)
             send(kept, there * 2 + core)
             send(given, there * 2 + other)
-            return carry
-
-        lax.fori_loop(1, CHIPS, go, 0)
         send(given, partner_row)
         got[row] = kept[0]
 

time: 90.3 us -> 90 us (level)
  no operation moved by 1% of the time
where the time goes in v4:
time: 90 us; the launch traced here: 88.8 us
  Pallas kernels  88.2 us (98%)
    pallas_call x1, Pallas kernels, shards(): pl.pallas_call(exchange, out_shape=[vmem(served, BF16)] * 3 + [vmem((2, J...  85.4 us
    pallas_call x1, Pallas kernels, shards(): pl.pallas_call(write_out, out_shape=[jax.ShapeDtypeStruct(served, BF16)]...  2.8 us

profile of v4, /device:TPU:2, one launch (start us, length us, event | category | flops | bytes accessed | tf_op | source)
XLA Modules:
  0.0 88.8 jit_solution(3129022297964914932)
XLA Ops:
  0.6 85.4 %exchange.1 = (bf16[16,32,2048]{2,1,0:T(8,128)(2,1)S(1)}, bf16[16,32,2048]{2,1,0:T(8,128)(2,1)S(1)}, bf16[16,32,2048]{2,1,0:T(8,128)(2,1)S(1)}, f32[2,24,1,128]{3,2,1,0:T(1,128)S(1)}, bf16[64,2048]{1,0:T(8,128)(2,1)S(1)}) custom-call(f32[16,64,1024]{2,1,0:T(8,128)} %refs_0_.1, bf16[16,64,1024]{2,1,0:T(8,128)(2,1)} %refs_1_.1, f32[16,64,1024]{2,1,0:T(8,128)} %refs_2_.1, ...), custom_call_target="tpu_custom_call" | custom-call | tf_op jit(solution)/shard_map/exchange/pallas_call | solution.py:404
  86.0 2.8 %write_out.1 = (bf16[16,32,2048]{2,1,0:T(8,128)(2,1)}, bf16[16,32,2048]{2,1,0:T(8,128)(2,1)}, bf16[16,32,2048]{2,1,0:T(8,128)(2,1)}, f32[16,32]{1,0:T(8,128)}, f...) custom-call(bf16[16,32,2048]{2,1,0:T(8,128)(2,1)S(1)} %get-tuple-element.19.refs_0_, ...), custom_call_target="tpu_custom_call" | custom-call | tf_op jit(solution)/shard_map/write_out/pallas_call | solution.py:435
